TPU v7x, 512 devices: a whole 4x8x8 slice. The times are simulated.
512 devices in a mesh: tm: 32 (over z, x), space: 16 (over y, core).
Axes of the slice: x: 4, y: 8, z: 8, core: 2. Of those that a mesh axis runs over, the one named last changes fastest.
Arguments:
- snapshots: bfloat16 [4096, 73728], P('tm', 'space'), may hold values from -12 to 12
- start_block: float32 [4096, 20], P('tm'), may hold values from -6 to 6
- merge_mix: float32 [40, 20], replicated, may hold values from -1 to 1
Outputs:
- modes: float32 [20, 73728], P(None, ('space', 'tm'))
- spectrum: float32 [20], replicated
All inputs are finite; a program needn't handle non-finite values.
Results may differ from a plain program's by a relative error of at most 0.012.
Values sent between devices are 32-bit elements; how exact they have to be, the bound alone decides.
A program may use at most 64 MiB of HBM per device.

v0:
```python
import math

import jax
import jax.numpy as jnp
from jax import lax
from jax.sharding import PartitionSpec as P

ITERS = 2


HIGHEST_PREC = lax.Precision.HIGHEST


def from_everyone(x, axis):
    devices = lax.axis_size(axis)
    return lax.all_to_all(jnp.broadcast_to(x[None], (devices, *x.shape)), axis, 0, 0, tiled=True)


def taken_together(x, axis):
    return from_everyone(x, axis).sum(axis=0)


def in_one(arrays, axis):
    ravelled, at, finished = (jnp.concatenate([a.reshape(-1) for a in arrays]), 0, [])
    so_far = taken_together(ravelled, axis)
    for a in arrays:
        finished.append(so_far[at : at + a.size].reshape(a.shape))
        at += a.size
    return tuple(finished)


def from_partner(block, axis, distance):
    count = lax.axis_size(axis)
    route = []
    for low in range(count):
        high = low | 1 << distance
        if high != low and high < count:
            route += [(low, high), (high, low)]
    return lax.ppermute(block, axis, route)


def merge_rule(gram_mat, mixing):
    weighted = jnp.dot(gram_mat, mixing, precision=HIGHEST_PREC)
    small_gram = jnp.dot(mixing.T, weighted, precision=HIGHEST_PREC)
    cholesky_low = jnp.linalg.cholesky(small_gram)
    coef_map = jax.scipy.linalg.solve_triangular(cholesky_low, mixing.T, lower=True)
    spread = jnp.dot(coef_map, gram_mat, precision=HIGHEST_PREC)
    singular = jnp.sqrt(jnp.sum(spread * spread, axis=1))
    return (coef_map, singular)


def local(snapshots, start_block, merge_mix):
    width = snapshots.shape[1] * lax.axis_size("space")
    block_proj = start_block
    for rounds in range(ITERS):
        rounded = block_proj.astype(jnp.bfloat16)
        images = lax.dot_general(
            rounded, snapshots, (((0,), (0,)), ((), ())), preferred_element_type=jnp.float32
        )
        images_b = images.astype(jnp.bfloat16)
        gram_part = lax.dot_general(
            images_b, images_b, (((1,), (1,)), ((), ())), preferred_element_type=jnp.float32
        )
        proj_part = lax.dot_general(
            snapshots, images_b, (((1,), (1,)), ((), ())), preferred_element_type=jnp.float32
        )
        gram_mat, projected = in_one((gram_part, proj_part), "space")
        cholesky_low = jnp.linalg.cholesky(gram_mat)
        block_proj = jax.scipy.linalg.solve_triangular(cholesky_low, projected.T, lower=True).T
    singular = jnp.sqrt(jnp.sum(block_proj * block_proj, axis=0))
    basis_rows = jax.scipy.linalg.solve_triangular(
        cholesky_low, images_b.astype(jnp.float32), lower=True
    )
    factor = singular[:, None] * basis_rows
    tile_total = lax.axis_size("tm")
    depth_total = tile_total.bit_length() - 1
    tm_place = lax.axis_index("tm")
    for height in range(depth_total):
        partner = from_partner(factor, "tm", height)
        upper = tm_place >> height & 1 == 1
        first = jnp.where(upper, partner, factor)
        second = jnp.where(upper, factor, partner)
        stacked = jnp.concatenate([first, second], axis=0)
        gram_local = jnp.dot(stacked, stacked.T, precision=HIGHEST_PREC)
        gram_mat = taken_together(gram_local, "space")
        coef_map, singular = merge_rule(gram_mat, merge_mix)
        basis_rows = jnp.dot(coef_map, stacked, precision=HIGHEST_PREC)
        factor = singular[:, None] * basis_rows
    piece_cols = basis_rows.shape[1] // tile_total
    own_cols = lax.dynamic_slice_in_dim(basis_rows, tm_place * piece_cols, piece_cols, 1)
    modes = own_cols * math.sqrt(width)
    spectrum = singular / math.sqrt(snapshots.shape[0] * width)
    return (modes, spectrum)


def solution(mesh):
    return jax.shard_map(
        local,
        mesh=mesh,
        in_specs=(P("tm", "space"), P("tm", None), P()),
        out_specs=(P(None, ("space", "tm")), P()),
        check_vma=False,
    )
```

profile of v0, /device:TPU:1, one launch (start us, length us, event | category | flops | bytes accessed | tf_op | source)
XLA Modules:
  0.0 250.4 jit_solution(9625613303907387255)
XLA Ops:
  0.6 1.3 copy-done
  1.9 1.0 convolution_convert_fusion.1
  4.0 19.5 %all_to_all.37 = f32[16,1,2960]{2,1,0:T(1,128)S(1)} all-to-all(f32[16,1,2960]{2,1,0:T(1,128)S(1)} %broadcast_in_dim.15), channel_id=1, replica_groups=mesh['tm'=32,'space'=16] {'space'}, dimensions={0} | all-to-all | bytes 378880 | tf_op jit(solution)/shard_map/all_to_all | solution.py:16
  23.9 1.8 cholesky.119
  26.4 0.6 fusion.14
  27.1 1.5 custom-call.18
  30.4 12.9 %all_to_all.38 = f32[16,1,2960]{2,1,0:T(1,128)S(1)} all-to-all(f32[16,1,2960]{2,1,0:T(1,128)S(1)} %broadcast_in_dim.16), channel_id=1, replica_groups=mesh['tm'=32,'space'=16] {'space'}, dimensions={0} | all-to-all | bytes 378880 | tf_op jit(solution)/shard_map/all_to_all | solution.py:16
  43.8 1.8 cholesky.130
  46.3 0.6 fusion.15
  46.9 1.5 custom-call.19
  49.4 2.2 collective-permute-start
  51.6 11.6 %collective-permute-done = f32[20,4608]{1,0:T(8,128)S(1)} collective-permute-done((f32[20,4608]{1,0:T(8,128)S(1)}, f32[20,4608]{1,0:T(8,128)S(1)}, u32[]{:S(2)}, u32[]{:S(2)}) %collective-permute-start) | collective-permute-done | bytes 368672 | tf_op jit(solution)/shard_map/ppermute | solution.py:39
  63.3 0.7 fusion.11
  64.3 11.7 %all_to_all.39 = f32[16,1,1600]{2,1,0:T(1,128)S(1)} all-to-all(f32[16,1,1600]{2,1,0:T(1,128)S(1)} %reshape.115), channel_id=1, replica_groups=mesh['tm'=32,'space'=16] {'space'}, dimensions={0} | all-to-all | bytes 204800 | tf_op jit(solution)/shard_map/all_to_all | solution.py:16
  76.6 0.9 reduce.7
  78.1 1.8 cholesky.141
  81.3 1.5 custom-call.20
  83.9 3.8 %collective-permute-start.1 = (f32[20,4608]{1,0:T(8,128)S(1)}, f32[20,4608]{1,0:T(8,128)S(1)}, u32[]{:S(2)}, u32[]{:S(2)}) collective-permute-start(f32[20,4608]{1,0:T(8,128)S(1)} %convolution_multiply_fusion.3), channel_id=1, source_target_pairs={{0,32},{32,0},{16,48},{48,16},{64,96},{96,64},{80,112},{112,80},{1... | collective-permute-start | bytes 1105928 | tf_op jit(solution)/shard_map/ppermute | solution.py:39
  87.7 11.5 %collective-permute-done.1 = f32[20,4608]{1,0:T(8,128)S(1)} collective-permute-done((f32[20,4608]{1,0:T(8,128)S(1)}, f32[20,4608]{1,0:T(8,128)S(1)}, u32[]{:S(2)}, u32[]{:S(2)}) %collective-permute-start.1) | collective-permute-done | bytes 368672 | tf_op jit(solution)/shard_map/ppermute | solution.py:39
  99.2 0.7 fusion.10
  100.2 11.8 %all_to_all.40 = f32[16,1,1600]{2,1,0:T(1,128)S(1)} all-to-all(f32[16,1,1600]{2,1,0:T(1,128)S(1)} %reshape.117), channel_id=1, replica_groups=mesh['tm'=32,'space'=16] {'space'}, dimensions={0} | all-to-all | bytes 204800 | tf_op jit(solution)/shard_map/all_to_all | solution.py:16
  112.0 0.9 reduce.8
  113.6 1.8 cholesky.152
  116.7 1.5 custom-call.21
  119.3 3.1 %collective-permute-start.2 = (f32[20,4608]{1,0:T(8,128)S(1)}, f32[20,4608]{1,0:T(8,128)S(1)}, u32[]{:S(2)}, u32[]{:S(2)}) collective-permute-start(f32[20,4608]{1,0:T(8,128)S(1)} %convolution_multiply_fusion.2), channel_id=1, source_target_pairs={{0,64},{64,0},{16,80},{80,16},{32,96},{96,32},{48,112},{112,48},{1... | collective-permute-start | bytes 1105928 | tf_op jit(solution)/shard_map/ppermute | solution.py:39
  122.5 10.6 %collective-permute-done.2 = f32[20,4608]{1,0:T(8,128)S(1)} collective-permute-done((f32[20,4608]{1,0:T(8,128)S(1)}, f32[20,4608]{1,0:T(8,128)S(1)}, u32[]{:S(2)}, u32[]{:S(2)}) %collective-permute-start.2) | collective-permute-done | bytes 368672 | tf_op jit(solution)/shard_map/ppermute | solution.py:39
  133.1 0.7 fusion.9
  134.2 11.8 %all_to_all.41 = f32[16,1,1600]{2,1,0:T(1,128)S(1)} all-to-all(f32[16,1,1600]{2,1,0:T(1,128)S(1)} %reshape.119), channel_id=1, replica_groups=mesh['tm'=32,'space'=16] {'space'}, dimensions={0} | all-to-all | bytes 204800 | tf_op jit(solution)/shard_map/all_to_all | solution.py:16
  146.0 0.9 reduce.9
  147.5 1.8 cholesky.163
  150.7 1.5 custom-call.22
  153.3 5.6 %collective-permute-start.3 = (f32[20,4608]{1,0:T(8,128)S(1)}, f32[20,4608]{1,0:T(8,128)S(1)}, u32[]{:S(2)}, u32[]{:S(2)}) collective-permute-start(f32[20,4608]{1,0:T(8,128)S(1)} %convolution_multiply_fusion.1), channel_id=1, source_target_pairs={{0,128},{128,0},{16,144},{144,16},{32,160},{160,32},{48,176},{176,... | collective-permute-start | bytes 1105928 | tf_op jit(solution)/shard_map/ppermute | solution.py:39
  158.9 20.1 %collective-permute-done.3 = f32[20,4608]{1,0:T(8,128)S(1)} collective-permute-done((f32[20,4608]{1,0:T(8,128)S(1)}, f32[20,4608]{1,0:T(8,128)S(1)}, u32[]{:S(2)}, u32[]{:S(2)}) %collective-permute-start.3) | collective-permute-done | bytes 368672 | tf_op jit(solution)/shard_map/ppermute | solution.py:39
  179.0 0.7 fusion.8
  180.1 11.5 %all_to_all.42 = f32[16,1,1600]{2,1,0:T(1,128)S(1)} all-to-all(f32[16,1,1600]{2,1,0:T(1,128)S(1)} %reshape.121), channel_id=1, replica_groups=mesh['tm'=32,'space'=16] {'space'}, dimensions={0} | all-to-all | bytes 204800 | tf_op jit(solution)/shard_map/all_to_all | solution.py:16
  191.6 0.9 reduce.10
  193.2 1.8 cholesky.174
  196.3 1.5 custom-call.23
  198.9 8.4 %collective-permute-start.4 = (f32[20,4608]{1,0:T(8,128)S(1)}, f32[20,4608]{1,0:T(8,128)S(1)}, u32[]{:S(2)}, u32[]{:S(2)}) collective-permute-start(f32[20,4608]{1,0:T(8,128)S(1)} %convolution_multiply_fusion), channel_id=1, source_target_pairs={{0,256},{256,0},{16,272},{272,16},{32,288},{288,32},{48,304},{304,... | collective-permute-start | bytes 1105928 | tf_op jit(solution)/shard_map/ppermute | solution.py:39
  207.4 20.2 %collective-permute-done.4 = f32[20,4608]{1,0:T(8,128)S(1)} collective-permute-done((f32[20,4608]{1,0:T(8,128)S(1)}, f32[20,4608]{1,0:T(8,128)S(1)}, u32[]{:S(2)}, u32[]{:S(2)}) %collective-permute-start.4) | collective-permute-done | bytes 368672 | tf_op jit(solution)/shard_map/ppermute | solution.py:39
  227.7 0.7 fusion.7
  228.5 0.9 reshape.123
  229.4 3.8 %all-to-all-start.6 = ((f32[16,1,1600]{2,1,0:T(1,128)}), f32[16,1,1600]{2,1,0:T(1,128)S(1)}, u32[]{:S(2)}, u32[]{:S(2)}) async-start(f32[16,1,1600]{2,1,0:T(1,128)} %reshape.123), calls=%async_computation.6 | async-start | bytes 212992 | tf_op jit(solution)/shard_map/all_to_all | solution.py:16
  233.2 8.7 %all-to-all-done.6 = f32[16,1,1600]{2,1,0:T(1,128)S(1)} async-done(((f32[16,1,1600]{2,1,0:T(1,128)}), f32[16,1,1600]{2,1,0:T(1,128)S(1)}, u32[]{:S(2)}, u32[]{:S(2)}) %all-to-all-start.6) | async-done | bytes 102432 | tf_op jit(solution)/shard_map/all_to_all | solution.py:16
  241.9 0.9 reduce.11
  243.4 1.8 cholesky.185
  246.6 1.5 custom-call.24
  249.7 0.7 dynamic-slice_multiply_fusion
  (120 shorter events, 23.4 us)
Async XLA Ops:
  0.6 1.3 copy-start
  49.4 13.8 %collective-permute-start = (f32[20,4608]{1,0:T(8,128)S(1)}, f32[20,4608]{1,0:T(8,128)S(1)}, u32[]{:S(2)}, u32[]{:S(2)}) collective-permute-start(f32[20,4608]{1,0:T(8,128)S(1)} %convolution_multiply_fusion.4), channel_id=1, source_target_pairs={{0,16},{16,0},{32,48},{48,32},{64,80},{80,64},{96,112},{112,96},{1... | collective-permute-start | bytes 1105928 | tf_op jit(solution)/shard_map/ppermute | solution.py:39
  64.0 13.7 %copy-start.1 = (f32[40,20]{0,1:T(8,128)S(1)}, f32[40,20]{0,1:T(8,128)}, u32[]{:S(2)}) copy-start(f32[40,20]{0,1:T(8,128)} %param.10) | copy-start | bytes 9604
  83.9 15.2 %collective-permute-start.1 = (f32[20,4608]{1,0:T(8,128)S(1)}, f32[20,4608]{1,0:T(8,128)S(1)}, u32[]{:S(2)}, u32[]{:S(2)}) collective-permute-start(f32[20,4608]{1,0:T(8,128)S(1)} %convolution_multiply_fusion.3), channel_id=1, source_target_pairs={{0,32},{32,0},{16,48},{48,16},{64,96},{96,64},{80,112},{112,80},{1... | collective-permute-start | bytes 1105928 | tf_op jit(solution)/shard_map/ppermute | solution.py:39
  119.3 13.7 %collective-permute-start.2 = (f32[20,4608]{1,0:T(8,128)S(1)}, f32[20,4608]{1,0:T(8,128)S(1)}, u32[]{:S(2)}, u32[]{:S(2)}) collective-permute-start(f32[20,4608]{1,0:T(8,128)S(1)} %convolution_multiply_fusion.2), channel_id=1, source_target_pairs={{0,64},{64,0},{16,80},{80,16},{32,96},{96,32},{48,112},{112,48},{1... | collective-permute-start | bytes 1105928 | tf_op jit(solution)/shard_map/ppermute | solution.py:39
  153.3 25.7 %collective-permute-start.3 = (f32[20,4608]{1,0:T(8,128)S(1)}, f32[20,4608]{1,0:T(8,128)S(1)}, u32[]{:S(2)}, u32[]{:S(2)}) collective-permute-start(f32[20,4608]{1,0:T(8,128)S(1)} %convolution_multiply_fusion.1), channel_id=1, source_target_pairs={{0,128},{128,0},{16,144},{144,16},{32,160},{160,32},{48,176},{176,... | collective-permute-start | bytes 1105928 | tf_op jit(solution)/shard_map/ppermute | solution.py:39
  198.9 28.7 %collective-permute-start.4 = (f32[20,4608]{1,0:T(8,128)S(1)}, f32[20,4608]{1,0:T(8,128)S(1)}, u32[]{:S(2)}, u32[]{:S(2)}) collective-permute-start(f32[20,4608]{1,0:T(8,128)S(1)} %convolution_multiply_fusion), channel_id=1, source_target_pairs={{0,256},{256,0},{16,272},{272,16},{32,288},{288,32},{48,304},{304,... | collective-permute-start | bytes 1105928 | tf_op jit(solution)/shard_map/ppermute | solution.py:39
  229.4 12.5 %all-to-all-start.6 = ((f32[16,1,1600]{2,1,0:T(1,128)}), f32[16,1,1600]{2,1,0:T(1,128)S(1)}, u32[]{:S(2)}, u32[]{:S(2)}) async-start(f32[16,1,1600]{2,1,0:T(1,128)} %reshape.123), calls=%async_computation.6 | async-start | bytes 212992 | tf_op jit(solution)/shard_map/all_to_all | solution.py:16
where the time goes:
time: 251 us; the launch traced here: 250 us
  waiting for transfers between devices  82.7 us (33%)
  blocking collectives  79.3 us (32%)
  other arithmetic  39.4 us (16%)
  starting transfers between devices  26.9 us (11%)
  matrix products  13.9 us (6%)
  local copies, waits for them, and re-layouts  6.84 us (3%)
    all_to_all x6, blocking collectives, from_everyone(): lax.all_to_all(jnp.broadcast_to(x[None], (devices, *x.shape)), axis, 0, 0...  79.3 us
    ppermute x5, waiting for transfers between devices, from_partner(): return lax.ppermute(block, axis, route)  74 us
    ppermute x5, starting transfers between devices, from_partner(): return lax.ppermute(block, axis, route)  23.1 us
    another operation x15, other arithmetic, merge_rule(): cholesky_low = jnp.linalg.cholesky(small_gram)  12.5 us
    another operation x10, other arithmetic, merge_rule(): jax.scipy.linalg.solve_triangular(cholesky_low, mixing.T, lower=True)  10.9 us
    all_to_all x1, waiting for transfers between devices, from_everyone(): lax.all_to_all(jnp.broadcast_to(x[None], (devices, *x.shape)), axis, 0, 0...  8.67 us
  transfers between devices with their start and end apart: 6, of which 6 were waited for; matrix products, arithmetic and copies ran while one was open for 0% of the time, Pallas kernels for 0%

commit v1 on v0

v1 whole, which is shorter than its diff:
```python
import functools
import math

import jax
import jax.numpy as jnp
from jax import lax
from jax.experimental import pallas as pl
from jax.experimental.pallas import tpu as pltpu
from jax.sharding import PartitionSpec as P

MESH = pl.DeviceIdType.MESH
HIGH = lax.Precision.HIGHEST
F32 = jnp.float32
BF16 = jnp.bfloat16
R = 20
RP = 24
N_SPACE = 16
N_TM = 32
G1 = 8
G2 = 4
PIECE = 144
LOCAL = 4608
X_PARTS = 4
ITERS = 2
S_A, S_C, X1, A1, B1, C1, X2, A2, B2, C2 = range(10)


def dot(a, b):
    return lax.dot_general(a, b, (((1,), (0,)), ((), ())), precision=HIGH, preferred_element_type=F32)


def dot_t(a, b):
    return lax.dot_general(a, b, (((1,), (1,)), ((), ())), precision=HIGH, preferred_element_type=F32)


def roll(x, by, axis=-1):
    size = x.shape[axis]
    by = by % size
    return x if by == 0 else pltpu.roll(x, by, axis % x.ndim)


def iota(shape, axis):
    return lax.broadcasted_iota(jnp.int32, shape, axis)


def keep_lanes(x, low, high):
    lane = iota(x.shape, x.ndim - 1)
    return jnp.where((lane >= low) & (lane < high), x, 0.0)


def gram_columns(rows, vectors):
    return [jnp.sum(rows * vectors[..., k : k + 1, :], axis=-1, keepdims=True) for k in range(R)]


def eliminate(columns, augmented):
    columns = list(columns)
    augmented = list(augmented)
    row_c = iota(columns[0].shape, columns[0].ndim - 2)
    row_a = iota(augmented[0].shape, augmented[0].ndim - 2)
    for j in range(R):
        inv = lax.rsqrt(columns[j][..., j : j + 1, :])
        low = jnp.where(row_c > j, columns[j] * inv, 0.0)
        for k in range(j + 1, R):
            columns[k] = columns[k] - low * low[..., k : k + 1, :]
        for n, a in enumerate(augmented):
            top = a[..., j : j + 1, :] * inv
            augmented[n] = jnp.where(row_a == j, top, a - low * top)
    return augmented


def combine(wide, first, second):
    total = None
    for k in range(R):
        for block, at in ((first, k), (second, R + k)):
            term = wide[at] * block[..., k : k + 1, :]
            total = term if total is None else total + term
    return total


def merge(cross, cross_t, square_a, square_b, mix_t, wide, images):
    lane, row = iota((1, RP, 128), 2), iota((1, RP, 128), 1)
    top = jnp.where(lane == row, square_a, 0.0) + roll(cross, R)
    bottom = cross_t + jnp.where(lane == row + R, square_b, 0.0)
    weighted = combine(wide, top, bottom)
    done = eliminate(gram_columns(weighted, mix_t[None]), [weighted] + images)
    squares = jnp.sum(done[0] * done[0], axis=-1, keepdims=True)
    return done[1:], squares


def pack_first(gram):
    lane = iota((40, 256), 1)
    row = iota((40, 256), 0)
    out = []
    for half in range(2):
        mine = gram[40 * half : 40 * half + 40]
        other = gram[80 * half : 80 * half + 40]
        far = keep_lanes(roll(mine, -80), 0, 80)
        near = keep_lanes(roll(other, 40 - 80 * half), 80, 120)
        total = far + near
        for q in range(2):
            p = 2 * q + half
            block = gram[40 * p : 40 * p + 40]
            norm = jnp.sum(jnp.where(lane == row + 40 * p, block, 0.0), axis=1, keepdims=True)
            total = total + jnp.where(lane == 120 + q, norm, 0.0)
        out.append(total[:, :128])
    last = None
    for p in range(4):
        block = roll(gram[40 * p : 40 * p + RP], -R - R * p)
        block = keep_lanes(block, R * p, R * p + R)
        last = block if last is None else last + block
    out.append(jnp.where(iota((RP, 128), 0) < R, last[:, :128], 0.0))
    return jnp.concatenate(out, axis=0)


def small(x):
    keep = (iota(x.shape, x.ndim - 1) < R) & (iota(x.shape, x.ndim - 2) < R)
    return jnp.where(keep, x, 0.0)


def transposed(x):
    full = jnp.concatenate([x, jnp.zeros((128 - RP, 128), F32)], axis=0)
    return full.T[:RP]


def tall(x):
    return jnp.concatenate([x, jnp.zeros((128 - RP, 128), F32)], axis=0)


def pair_up(maps, squares, blocks, width, mix_t, wide, last=False):
    crosses, crosses_t, images = [], [], []
    for p, block in enumerate(blocks):
        a, b = maps[2 * p], maps[2 * p + 1]
        mid = keep_lanes(dot(a[:, :width], block), 0, width)
        crosses.append(small(dot_t(mid, tall(b))))
        crosses_t.append(small(dot_t(b, tall(mid))))
        images.append((dot(mix_t[:, :RP], a), dot(roll(mix_t, -R)[:, :RP], b)))
    stack = lambda seq: jnp.stack(seq, axis=0)
    if 2 * width <= 128:
        carried = [stack([x + roll(y, width) for x, y in images])]
    else:
        carried = [stack([x for x, _ in images]), stack([y for _, y in images])]
    sq_a = stack([squares[2 * p] for p in range(len(blocks))])
    sq_b = stack([squares[2 * p + 1] for p in range(len(blocks))])
    out, sq = merge(stack(crosses), stack(crosses_t), sq_a, sq_b, mix_t, wide, carried)
    if not last:
        scale = jnp.sqrt(sq)
        out = [x * scale for x in out]
    return out, sq


def base_level(crosses, norms, mix_t, wide):
    stack = lambda seq: jnp.stack(seq, axis=0)
    cross = stack(crosses)
    cross_t = stack([transposed(c) for c in crosses])
    images = jnp.broadcast_to(mix_t[None], cross.shape)
    out, sq = merge(cross, cross_t, stack(norms[0::2]), stack(norms[1::2]), mix_t, wide, [images])
    return out[0] * jnp.sqrt(sq), sq


def rows_of(squares):
    return jnp.where(iota(squares.shape, squares.ndim - 2) < R, squares, 0.0)


def first_stage(summed, norm_rows, mix_t, wide):
    last = summed[80 : 80 + RP]
    crosses = [small(roll(last, -R * p)) for p in range(4)]
    norms = [rows_of(norm_rows(R * (t % 4), 120 + t // 4)) for t in range(8)]
    maps, sq = base_level(crosses, norms, mix_t, wide)
    near = roll(summed[:80], -80)
    out, sq2 = pair_up([maps[p] for p in range(4)], [sq[p] for p in range(4)], [near[0:40], near[40:80]], 40, mix_t, wide)
    out, sq3 = pair_up([out[0][0], out[0][1]], [sq2[0], sq2[1]], [summed[0:80]], 80, mix_t, wide)
    return out[0][0], out[1][0]


def pack_second(gram):
    far = keep_lanes(roll(gram[0:40], -40), 0, 40)
    lane, row = iota((40, 128), 1), iota((40, 128), 0)
    total = far
    for p in range(2):
        block = gram[40 * p : 40 * p + 40]
        norm = jnp.sum(jnp.where(lane == row + 40 * p, block, 0.0), axis=1, keepdims=True)
        total = total + jnp.where(lane == 80 + p, norm, 0.0)
        near = keep_lanes(roll(block, 40 + R * p - 40 * p - R), 40 + R * p, 60 + R * p)
        total = total + jnp.where(row < R, near, 0.0)
    return total


def second_stage(summed, norm_rows, mix_t, wide):
    top = summed[0:RP]
    crosses = [small(roll(top, -40 - R * p)) for p in range(2)]
    norms = [rows_of(norm_rows(R * (t % 2), 80 + t // 2)) for t in range(4)]
    maps, sq = base_level(crosses, norms, mix_t, wide)
    out, sq2 = pair_up([maps[0], maps[1]], [sq[0], sq[1]], [summed[0:40]], 40, mix_t, wide, last=True)
    return out[0][0], sq2[0]


def first_pieces(factor):
    lane = iota((RP, 128), 1)
    for place in range(G1):
        windows = []
        for g in range(G2):
            at = 128 * (9 * g + place)
            windows.append(roll(factor(at), 16 * g - 16 * place))
        tiles = [windows[0][:, :128]]
        for g in range(1, G2):
            tiles.append(jnp.where(lane < 16 * g, windows[g - 1][:, 128:], windows[g][:, :128]))
        tiles.append(jnp.where(lane < 64, windows[3][:, 128:], 0.0))
        yield place, tiles


def split3(x):
    high = x.astype(BF16)
    rest = x - high.astype(F32)
    mid = rest.astype(BF16)
    low = (rest - mid.astype(F32)).astype(BF16)
    return high, mid, low


def tile_step(o_t, s_mat, extra):
    proj = dot(o_t, s_mat)
    return eliminate(gram_columns(proj, o_t), [proj] + extra)


def kernel(x_hbm, start_ref, mix_ref, modes_ref, spec_ref,
           xv, square, wide_ref, factor_ref, part_s, got_s, sum_s,
           out1, in1, slab1, part1, got1, mid1, sum1,
           wide2, out2, in2, slab2, part2, got2, mid2, sum2,
           load_sem, send_sem, recv_sem):
    tm = lax.axis_index("tm")
    sp = lax.axis_index("space")
    group, place = tm // G1, lax.rem(tm, G1)
    own_tile = sp // 2 + 8 * (1 - lax.rem(sp, 2))

    cols = LOCAL // X_PARTS
    loads = [
        pltpu.make_async_copy(x_hbm.at[:, pl.ds(cols * c, cols)], xv.at[:, pl.ds(cols * c, cols)], load_sem.at[c])
        for c in range(X_PARTS)
    ]
    for load in loads:
        load.start()

    barrier = pltpu.get_barrier_semaphore()

    def greet_space(d, carry):
        pl.semaphore_signal(barrier, inc=1, device_id=(tm, lax.rem(sp + d, N_SPACE)), device_id_type=MESH)
        return carry

    def greet_tm(d, carry):
        pl.semaphore_signal(barrier, inc=1, device_id=(lax.rem(tm + d, N_TM), sp), device_id_type=MESH)
        return carry

    lax.fori_loop(1, N_SPACE, greet_space, 0)
    lax.fori_loop(1, N_TM, greet_tm, 0)

    square[...] = jnp.zeros((128, 128), F32)
    square[:, 0:R] = start_ref[...]
    o_t = square[...].T[0:RP].astype(BF16).astype(F32)
    square[...] = jnp.zeros((128, 128), F32)
    square[0 : 2 * R, 0:R] = mix_ref[...]
    mix_t = square[...].T[0:RP]
    for k in range(2 * R):
        wide_ref[k] = jnp.broadcast_to(mix_t[:, k : k + 1], (RP, 128))
    slab1[...] = jnp.zeros(slab1.shape, F32)
    slab2[...] = jnp.zeros(slab2.shape, F32)
    wide = [wide_ref.at[k] for k in range(2 * R)]

    s_mat = jnp.zeros((128, 128), F32)
    for c in range(X_PARTS):
        loads[c].wait()
        block = xv[:, cols * c : cols * (c + 1)]
        s_mat = s_mat + lax.dot_general(block, block, (((1,), (1,)), ((), ())), preferred_element_type=F32)
    part_s[...] = s_mat.reshape(16, 8, 128)

    pl.semaphore_wait(barrier, N_SPACE - 1 + N_TM - 1)

    def rounds(first, last, make):
        def go(d, carry):
            make(d, lambda copy: copy.start())
            return carry

        def end(d, carry):
            make(d, lambda copy: copy.wait_send())
            return carry

        return lambda: lax.fori_loop(first, last, go, 0), lambda: lax.fori_loop(first, last, end, 0)

    def arrived(ref, count, phase):
        some = ref.at[pl.ds(0, count)]
        pltpu.make_async_copy(some, some, recv_sem.at[phase]).wait()

    def send(src, dst, d, phase, tm_to, sp_to):
        return pltpu.make_async_remote_copy(
            src_ref=src, dst_ref=dst, send_sem=send_sem.at[d], recv_sem=recv_sem.at[phase],
            device_id=(tm_to, sp_to), device_id_type=MESH)

    def all_reduce(part, got, mid, total, tiles, phases, tm_count, tm_place, tm_peer):
        phase_a, phase_b, phase_c = phases

        def scatter(d, act):
            peer = lax.rem(sp + d, N_SPACE)
            tile = peer // 2 + 8 * (1 - lax.rem(peer, 2))

            @pl.when(tile < tiles)
            def _():
                act(send(part.at[tile], got.at[sp], d, phase_a, tm, peer))

        def across(d, act):
            act(send(mid.at[tm_place], mid.at[tm_place], d, phase_b, tm_peer(d), sp))

        def gather(d, act):
            act(send(total.at[own_tile], total.at[own_tile], d, phase_c, tm, lax.rem(sp + d, N_SPACE)))

        go, end = rounds(1, N_SPACE, scatter)
        go()

        @pl.when(own_tile < tiles)
        def _():
            got[sp] = part[own_tile]
            arrived(got, N_SPACE - 1, phase_a)
            acc = jnp.sum(got[...], axis=0)
            end()
            if tm_count > 1:
                mid[tm_place] = acc
                go_b, end_b = rounds(1, tm_count, across)
                go_b()
                arrived(mid, tm_count - 1, phase_b)
                acc = jnp.sum(mid[...], axis=0)
                end_b()
            total[own_tile] = acc
            go_c, end_c = rounds(1, N_SPACE, gather)
            go_c()
            arrived(total, tiles - 1, phase_c)
            end_c()

        @pl.when(own_tile >= tiles)
        def _():
            end()
            arrived(total, tiles, phase_c)

    all_reduce(part_s, got_s, None, sum_s, 16, (S_A, None, S_C), 1, None, None)
    s_mat = sum_s[...].reshape(128, 128)

    eye = jnp.where(iota((RP, 128), 0) == iota((RP, 128), 1), 1.0, 0.0)
    for step in range(ITERS):
        if step:
            o_t = o_t.astype(BF16).astype(F32)
        last_block = o_t
        o_t, *inverse = tile_step(o_t, s_mat, [eye] if step == ITERS - 1 else [])
    scale = jnp.sqrt(jnp.sum(o_t * o_t, axis=1, keepdims=True))
    weights = jnp.concatenate(split3(jnp.concatenate([inverse[0] * scale, jnp.zeros((32 - RP, 128), F32)], axis=0)[:, :32]), axis=0)
    block = jnp.concatenate([last_block, jnp.zeros((32 - RP, 128), F32)], axis=0).astype(BF16)
    for c in range(X_PARTS):
        at = slice(cols * c, cols * (c + 1))
        image = jnp.dot(block, xv[:, at], preferred_element_type=F32).astype(BF16)
        three = jnp.dot(weights, image, preferred_element_type=F32)
        factor_ref[:, at] = (three[0:RP] + three[32 : 32 + RP]) + three[64 : 64 + RP]

    for there, tiles in first_pieces(lambda at: factor_ref[:, at : at + 256]):
        for c, t in enumerate(tiles):
            out1[there, :, 128 * c : 128 * (c + 1)] = t[0:R]

    def exchange1(d, act):
        there = lax.rem(place + d, G1)
        act(send(out1.at[there], in1.at[place], d, X1, G1 * group + there, sp))

    go, end = rounds(1, G1, exchange1)
    go()
    in1[place] = out1[place]
    arrived(in1, G1 - 1, X1)
    end()
    for t in range(G1):
        slab1[R * t : R * t + R, :] = in1[t]
    rows = slab1[0 : R * G1]
    gram = dot_t(rows, slab1[...])
    part1[...] = jnp.concatenate([pack_first(gram), jnp.zeros((24, 128), F32)], axis=0).reshape(16, 8, 128)
    all_reduce(part1, got1, mid1, sum1, 13, (A1, B1, C1), G1, place, lambda d: G1 * group + lax.rem(place + d, G1))
    square[0:104] = sum1[0:13].reshape(104, 128)
    left, right = first_stage(square[...], lambda row, lane: square[row : row + RP, :][:, lane : lane + 1], mix_t, wide_ref[...])
    merged = dot(left[:, :80], slab1[0:80]) + dot(right[:, :80], slab1[80:160])
    wide2[...] = merged

    for g in range(G2):
        window = keep_lanes(roll(wide2[:, 128 * g : 128 * g + 256], -16 * g), 0, PIECE)
        out2[g] = window[0:R]

    def exchange2(d, act):
        there = lax.rem(group + d, G2)
        act(send(out2.at[there], in2.at[group], d, X2, G1 * there + place, sp))

    go, end = rounds(1, G2, exchange2)
    go()
    in2[group] = out2[group]
    arrived(in2, G2 - 1, X2)
    end()
    for t in range(G2):
        slab2[R * t : R * t + R, :] = in2[t]
    gram = dot_t(slab2[0:80], slab2[...])
    part2[0:5] = pack_second(gram).reshape(5, 8, 128)
    all_reduce(part2, got2, mid2, sum2, 5, (A2, B2, C2), N_TM, tm, lambda d: lax.rem(tm + d, N_TM))
    square[0:40] = sum2[0:5].reshape(40, 128)
    coef, squares = second_stage(square[...], lambda row, lane: square[row : row + RP, :][:, lane : lane + 1], mix_t, wide_ref[...])
    final = dot(coef[:, :80], slab2[0:80]) * math.sqrt(LOCAL * N_SPACE)
    modes_ref[...] = final[0:R, 0:PIECE]
    values = jnp.sqrt(squares) * (1.0 / math.sqrt(128 * LOCAL * N_SPACE))
    spec_ref[...] = jnp.sum(eye * values, axis=0, keepdims=True)[:, 0:R]


def local(snapshots, start_block, merge_mix):
    vmem = pl.BlockSpec(memory_space=pltpu.VMEM)
    tile16 = pltpu.VMEM((16, 8, 128), F32)
    modes, spectrum = pl.pallas_call(
        kernel,
        out_shape=(jax.ShapeDtypeStruct((R, PIECE), F32), jax.ShapeDtypeStruct((1, R), F32)),
        in_specs=[pl.BlockSpec(memory_space=pl.ANY), vmem, vmem],
        out_specs=(vmem, vmem),
        scratch_shapes=[
            pltpu.VMEM((128, LOCAL), BF16),
            pltpu.VMEM((128, 128), F32),
            pltpu.VMEM((2 * R, RP, 128), F32),
            pltpu.VMEM((RP, LOCAL), F32),
            tile16, tile16, tile16,
            pltpu.VMEM((G1, R, 640), F32),
            pltpu.VMEM((G1, R, 640), F32),
            pltpu.VMEM((256, 640), F32),
            tile16, tile16, pltpu.VMEM((G1, 8, 128), F32), tile16,
            pltpu.VMEM((RP, 640), F32),
            pltpu.VMEM((G2, R, 256), F32),
            pltpu.VMEM((G2, R, 256), F32),
            pltpu.VMEM((128, 256), F32),
            tile16, tile16, pltpu.VMEM((N_TM, 8, 128), F32), tile16,
            pltpu.SemaphoreType.DMA((X_PARTS,)),
            pltpu.SemaphoreType.DMA((N_TM,)),
            pltpu.SemaphoreType.DMA((10,)),
        ],
        compiler_params=pltpu.CompilerParams(collective_id=0, has_side_effects=True),
    )(snapshots, start_block, merge_mix)
    return modes, spectrum.reshape(R)


def solution(mesh):
    return jax.shard_map(
        local,
        mesh=mesh,
        in_specs=(P("tm", "space"), P("tm", None), P()),
        out_specs=(P(None, ("space", "tm")), P()),
        check_vma=False,
    )
```

time: 251 us -> 86.4 us (0.34)
  waiting for transfers between devices: 82.7 us -> 0 us
  Pallas kernels: 0 us -> 80.1 us
  blocking collectives: 79.3 us -> 0 us
  other arithmetic: 39.4 us -> 0 us
  starting transfers between devices: 26.9 us -> 0 us
  matrix products: 13.9 us -> 0 us
    pallas_call x0 -> x1, Pallas kernels: none -> 80.1 us  [local(): pl.pallas_call(kernel, out_shape=(jax.ShapeDtypeStruct((R, PIECE), F32),...]
    all_to_all x6 -> x0, blocking collectives: 79.3 us -> none  [from_everyone(): lax.all_to_all(jnp.broadcast_to(x[None], (devices, *x.shape)), axis, 0, 0...]
    ppermute x5 -> x0, waiting for transfers between devices: 74 us -> none  [from_partner(): return lax.ppermute(block, axis, route)]
    another operation x35 -> x0, other arithmetic: 32.8 us -> none  [the longest x15 12.5 us: merge_rule(): cholesky_low = jnp.linalg.cholesky(small_gram)]
    ppermute x5 -> x0, starting transfers between devices: 23.1 us -> none  [from_partner(): return lax.ppermute(block, axis, route)]
    dot_general x31 -> x0, matrix products: 11.8 us -> none  [the longest x5 3.6 us: local(): gram_local = jnp.dot(stacked, stacked.T, precision=HIGHEST_PREC)]
    all_to_all x1 -> x0, waiting for transfers between devices: 8.67 us -> none  [from_everyone(): lax.all_to_all(jnp.broadcast_to(x[None], (devices, *x.shape)), axis, 0, 0...]
    all_to_all x5 -> x0, other arithmetic: 4.5 us -> none  [from_everyone(): lax.all_to_all(jnp.broadcast_to(x[None], (devices, *x.shape)), axis, 0, 0...]
  transfers between devices with their start and end apart: 6 -> 0, of which waited for: 6 -> 0; matrix products, arithmetic and copies ran while one was open for 0% -> 0% of each run, Pallas kernels for 0% -> 0%
where the time goes in v1:
time: 86.4 us; the launch traced here: 86.1 us
  Pallas kernels  80.1 us (93%)
  local copies, waits for them, and re-layouts  5.35 us (6%)
    pallas_call x1, Pallas kernels, local(): pl.pallas_call(kernel, out_shape=(jax.ShapeDtypeStruct((R, PIECE), F32),...  80.1 us
    unnamed x4, local copies, waits for them, and re-layouts  5.35 us

profile of v1, /device:TPU:1, one launch (start us, length us, event | category | flops | bytes accessed | tf_op | source)
XLA Modules:
  0.0 86.1 jit_solution(16128650982642963281)
XLA Ops:
  0.6 1.4 %copy.6.mix_ref = f32[40,20]{1,0:T(8,128)} copy(f32[40,20]{0,1:T(8,128)} %param.5) | data formatting | bytes 6400 | tf_op args[2]
  2.0 1.4 %copy.5.start_ref = f32[128,20]{1,0:T(8,128)} copy(f32[128,20]{0,1:T(8,128)} %param.4) | data formatting | bytes 20480 | tf_op args[1]
  3.4 80.1 %shard_map.50 = (f32[20,144]{1,0:T(8,128)}, f32[1,20]{1,0:T(1,128)}) custom-call(bf16[128,4608]{1,0:T(8,128)(2,1)} %x_hbm.1, f32[128,20]{1,0:T(8,128)} %copy.5.start_ref, f32[40,20]{1,0:T(8,128)} %copy.6.mix_ref), custom_call_target="tpu_custom_call" | custom-call | tf_op jit(solution)/shard_map/pallas_call | solution.py:411
  83.5 1.3 %copy.9 = f32[20,144]{1,0:T(8,128)} copy(f32[20,144]{1,0:T(8,128)} %get-tuple-element.8) | data formatting | bytes 23040
  84.9 1.2 %copy.10 = f32[20]{0:T(128)} copy(f32[20]{0:T(128)} %bitcast.1) | data formatting | bytes 160

commit v2 on v1

--- a/solution.py
+++ b/solution.py
@@ -22,6 +22,9 @@
 LOCAL = 4608
 X_PARTS = 4
 ITERS = 2
+FAR8 = (4, 3, 5, 2, 6, 1, 7)
+FAR_ZX = sorted(((dz, dx) for dz in range(8) for dx in range(4) if dz or dx), key=lambda d: -(min(d[0], 8 - d[0]) + min(d[1], 4 - d[1])))
+FAR_GROUP = ((1, 2), (1, 1), (1, 3), (0, 2), (1, 0), (0, 1), (0, 3))
 S_A, S_C, X1, A1, B1, C1, X2, A2, B2, C2 = range(10)
 
 
@@ -49,23 +52,32 @@
 
 
 def gram_columns(rows, vectors):
-    return [jnp.sum(rows * vectors[..., k : k + 1, :], axis=-1, keepdims=True) for k in range(R)]
+    return [
+        jnp.sum(rows[..., k // 8 * 8 :, :] * vectors[..., k : k + 1, :], axis=-1, keepdims=True) for k in range(R)
+    ]
 
 
 def eliminate(columns, augmented):
     columns = list(columns)
     augmented = list(augmented)
-    row_c = iota(columns[0].shape, columns[0].ndim - 2)
-    row_a = iota(augmented[0].shape, augmented[0].ndim - 2)
+    finished = [[] for _ in augmented]
     for j in range(R):
-        inv = lax.rsqrt(columns[j][..., j : j + 1, :])
-        low = jnp.where(row_c > j, columns[j] * inv, 0.0)
+        start = j // 8 * 8
+        if j and j == start:
+            for n, a in enumerate(augmented):
+                finished[n].append(a[..., :8, :])
+                augmented[n] = a[..., 8:, :]
+        here = columns[j]
+        at = j - start
+        inv = lax.rsqrt(here[..., at : at + 1, :])
+        low = jnp.where(iota(here.shape, here.ndim - 2) > at, here * inv, 0.0)
         for k in range(j + 1, R):
-            columns[k] = columns[k] - low * low[..., k : k + 1, :]
+            begin = k // 8 * 8
+            columns[k] = columns[k] - low[..., begin - start :, :] * low[..., k - start : k - start + 1, :]
         for n, a in enumerate(augmented):
-            top = a[..., j : j + 1, :] * inv
-            augmented[n] = jnp.where(row_a == j, top, a - low * top)
-    return augmented
+            top = a[..., at : at + 1, :] * inv
+            augmented[n] = jnp.where(iota(a.shape, a.ndim - 2) == at, top, a - low * top)
+    return [jnp.concatenate(done + [a], axis=-2) for done, a in zip(finished, augmented)]
 
 
 def combine(wide, first, second):
@@ -221,7 +233,7 @@
     return eliminate(gram_columns(proj, o_t), [proj] + extra)
 
 
-def kernel(x_hbm, start_ref, mix_ref, modes_ref, spec_ref,
+def kernel(x_hbm, start_ref, mix_ref, out_ref,
            xv, square, wide_ref, factor_ref, part_s, got_s, sum_s,
            out1, in1, slab1, part1, got1, mid1, sum1,
            wide2, out2, in2, slab2, part2, got2, mid2, sum2,
@@ -229,7 +241,8 @@
     tm = lax.axis_index("tm")
     sp = lax.axis_index("space")
     group, place = tm // G1, lax.rem(tm, G1)
-    own_tile = sp // 2 + 8 * (1 - lax.rem(sp, 2))
+    y, core = sp // 2, lax.rem(sp, 2)
+    z, x = tm // 4, lax.rem(tm, 4)
 
     cols = LOCAL // X_PARTS
     loads = [
@@ -253,11 +266,11 @@
     lax.fori_loop(1, N_TM, greet_tm, 0)
 
     square[...] = jnp.zeros((128, 128), F32)
-    square[:, 0:R] = start_ref[...]
-    o_t = square[...].T[0:RP].astype(BF16).astype(F32)
-    square[...] = jnp.zeros((128, 128), F32)
-    square[0 : 2 * R, 0:R] = mix_ref[...]
-    mix_t = square[...].T[0:RP]
+    square[0:R] = start_ref[...]
+    o_t = square[0:RP].astype(BF16).astype(F32)
+    square[0:R] = jnp.zeros((R, 128), F32)
+    square[0:R, 0 : 2 * R] = mix_ref[...]
+    mix_t = square[0:RP]
     for k in range(2 * R):
         wide_ref[k] = jnp.broadcast_to(mix_t[:, k : k + 1], (RP, 128))
     slab1[...] = jnp.zeros(slab1.shape, F32)
@@ -269,20 +282,15 @@
         loads[c].wait()
         block = xv[:, cols * c : cols * (c + 1)]
         s_mat = s_mat + lax.dot_general(block, block, (((1,), (1,)), ((), ())), preferred_element_type=F32)
-    part_s[...] = s_mat.reshape(16, 8, 128)
+    part_s[...] = s_mat.reshape(8, 16, 128)
 
     pl.semaphore_wait(barrier, N_SPACE - 1 + N_TM - 1)
 
-    def rounds(first, last, make):
-        def go(d, carry):
-            make(d, lambda copy: copy.start())
-            return carry
-
-        def end(d, carry):
-            make(d, lambda copy: copy.wait_send())
-            return carry
-
-        return lambda: lax.fori_loop(first, last, go, 0), lambda: lax.fori_loop(first, last, end, 0)
+    def start(copy):
+        copy.start()
+
+    def sent(copy):
+        copy.wait_send()
 
     def arrived(ref, count, phase):
         some = ref.at[pl.ds(0, count)]
@@ -293,51 +301,56 @@
             src_ref=src, dst_ref=dst, send_sem=send_sem.at[d], recv_sem=recv_sem.at[phase],
             device_id=(tm_to, sp_to), device_id_type=MESH)
 
-    def all_reduce(part, got, mid, total, tiles, phases, tm_count, tm_place, tm_peer):
+    def all_reduce(part, got, mid, total, phases, tm_place, tm_peers):
         phase_a, phase_b, phase_c = phases
-
-        def scatter(d, act):
-            peer = lax.rem(sp + d, N_SPACE)
-            tile = peer // 2 + 8 * (1 - lax.rem(peer, 2))
-
-            @pl.when(tile < tiles)
-            def _():
-                act(send(part.at[tile], got.at[sp], d, phase_a, tm, peer))
-
-        def across(d, act):
-            act(send(mid.at[tm_place], mid.at[tm_place], d, phase_b, tm_peer(d), sp))
-
-        def gather(d, act):
-            act(send(total.at[own_tile], total.at[own_tile], d, phase_c, tm, lax.rem(sp + d, N_SPACE)))
-
-        go, end = rounds(1, N_SPACE, scatter)
-        go()
-
-        @pl.when(own_tile < tiles)
+        owners = part.shape[0]
+        mine = (core == 1) & (y < owners)
+
+        def scatter(act):
+            for n, dy in enumerate(FAR8 + (0,)):
+                to = lax.rem(y + dy, 8)
+
+                @pl.when((to < owners) & (core == 0) if dy == 0 else to < owners)
+                def _():
+                    act(send(part.at[to], got.at[sp], n, phase_a, tm, 2 * to + 1))
+
+        def across(act):
+            for n, to in enumerate(tm_peers):
+                act(send(mid.at[tm_place], mid.at[tm_place], n, phase_b, to, sp))
+
+        def gather(act):
+            for n, dy in enumerate(FAR8):
+                for c in range(2):
+                    act(send(total.at[y], total.at[y], 2 * n + c, phase_c, tm, 2 * lax.rem(y + dy, 8) + c))
+            act(send(total.at[y], total.at[y], 14, phase_c, tm, 2 * y))
+
+        scatter(start)
+
+        @pl.when(mine)
         def _():
-            got[sp] = part[own_tile]
+            got[sp] = part[y]
             arrived(got, N_SPACE - 1, phase_a)
             acc = jnp.sum(got[...], axis=0)
-            end()
-            if tm_count > 1:
+            if tm_peers:
+                scatter(sent)
                 mid[tm_place] = acc
-                go_b, end_b = rounds(1, tm_count, across)
-                go_b()
-                arrived(mid, tm_count - 1, phase_b)
+                across(start)
+                arrived(mid, len(tm_peers), phase_b)
                 acc = jnp.sum(mid[...], axis=0)
-                end_b()
-            total[own_tile] = acc
-            go_c, end_c = rounds(1, N_SPACE, gather)
-            go_c()
-            arrived(total, tiles - 1, phase_c)
-            end_c()
-
-        @pl.when(own_tile >= tiles)
+                across(sent)
+            total[y] = acc
+            if not tm_peers:
+                scatter(sent)
+            gather(start)
+            arrived(total, owners - 1, phase_c)
+            gather(sent)
+
+        @pl.when(jnp.logical_not(mine))
         def _():
-            end()
-            arrived(total, tiles, phase_c)
-
-    all_reduce(part_s, got_s, None, sum_s, 16, (S_A, None, S_C), 1, None, None)
+            scatter(sent)
+            arrived(total, owners, phase_c)
+
+    all_reduce(part_s, got_s, None, sum_s, (S_A, None, S_C), None, ())
     s_mat = sum_s[...].reshape(128, 128)
 
     eye = jnp.where(iota((RP, 128), 0) == iota((RP, 128), 1), 1.0, 0.0)
@@ -359,22 +372,23 @@
         for c, t in enumerate(tiles):
             out1[there, :, 128 * c : 128 * (c + 1)] = t[0:R]
 
-    def exchange1(d, act):
-        there = lax.rem(place + d, G1)
-        act(send(out1.at[there], in1.at[place], d, X1, G1 * group + there, sp))
-
-    go, end = rounds(1, G1, exchange1)
-    go()
+    near = [lax.rem(place // 4 + dz, 2) * 4 + lax.rem(x + dx, 4) for dz, dx in FAR_GROUP]
+
+    def exchange1(act):
+        for n, there in enumerate(near):
+            act(send(out1.at[there], in1.at[place], n, X1, G1 * group + there, sp))
+
+    exchange1(start)
     in1[place] = out1[place]
     arrived(in1, G1 - 1, X1)
-    end()
+    exchange1(sent)
     for t in range(G1):
         slab1[R * t : R * t + R, :] = in1[t]
     rows = slab1[0 : R * G1]
     gram = dot_t(rows, slab1[...])
-    part1[...] = jnp.concatenate([pack_first(gram), jnp.zeros((24, 128), F32)], axis=0).reshape(16, 8, 128)
-    all_reduce(part1, got1, mid1, sum1, 13, (A1, B1, C1), G1, place, lambda d: G1 * group + lax.rem(place + d, G1))
-    square[0:104] = sum1[0:13].reshape(104, 128)
+    part1[...] = jnp.concatenate([pack_first(gram), jnp.zeros((8, 128), F32)], axis=0).reshape(7, 16, 128)
+    all_reduce(part1, got1, mid1, sum1, (A1, B1, C1), place, [G1 * group + there for there in near])
+    square[0:112] = sum1[...].reshape(112, 128)
     left, right = first_stage(square[...], lambda row, lane: square[row : row + RP, :][:, lane : lane + 1], mix_t, wide_ref[...])
     merged = dot(left[:, :80], slab1[0:80]) + dot(right[:, :80], slab1[80:160])
     wide2[...] = merged
@@ -383,57 +397,69 @@
         window = keep_lanes(roll(wide2[:, 128 * g : 128 * g + 256], -16 * g), 0, PIECE)
         out2[g] = window[0:R]
 
-    def exchange2(d, act):
-        there = lax.rem(group + d, G2)
-        act(send(out2.at[there], in2.at[group], d, X2, G1 * there + place, sp))
-
-    go, end = rounds(1, G2, exchange2)
-    go()
+    def exchange2(act):
+        for n, dg in enumerate((2, 1, 3)):
+            there = lax.rem(group + dg, G2)
+            act(send(out2.at[there], in2.at[group], n, X2, G1 * there + place, sp))
+
+    exchange2(start)
     in2[group] = out2[group]
     arrived(in2, G2 - 1, X2)
-    end()
+    exchange2(sent)
     for t in range(G2):
         slab2[R * t : R * t + R, :] = in2[t]
     gram = dot_t(slab2[0:80], slab2[...])
-    part2[0:5] = pack_second(gram).reshape(5, 8, 128)
-    all_reduce(part2, got2, mid2, sum2, 5, (A2, B2, C2), N_TM, tm, lambda d: lax.rem(tm + d, N_TM))
-    square[0:40] = sum2[0:5].reshape(40, 128)
+    part2[...] = pack_second(gram).reshape(5, 8, 128)
+    everyone = [lax.rem(z + dz, 8) * 4 + lax.rem(x + dx, 4) for dz, dx in FAR_ZX]
+    all_reduce(part2, got2, mid2, sum2, (A2, B2, C2), tm, everyone)
+    square[0:40] = sum2[...].reshape(40, 128)
     coef, squares = second_stage(square[...], lambda row, lane: square[row : row + RP, :][:, lane : lane + 1], mix_t, wide_ref[...])
     final = dot(coef[:, :80], slab2[0:80]) * math.sqrt(LOCAL * N_SPACE)
-    modes_ref[...] = final[0:R, 0:PIECE]
+    out_ref[0:RP] = final
     values = jnp.sqrt(squares) * (1.0 / math.sqrt(128 * LOCAL * N_SPACE))
-    spec_ref[...] = jnp.sum(eye * values, axis=0, keepdims=True)[:, 0:R]
+    out_ref[RP : RP + 1, 0:128] = jnp.sum(eye * values, axis=0, keepdims=True)
+
+
+def write_out(result_ref, modes_ref, spec_ref):
+    modes_ref[...] = result_ref[0:R, 0:PIECE]
+    spec_ref[...] = result_ref[RP : RP + 1, 0:R]
 
 
 def local(snapshots, start_block, merge_mix):
     vmem = pl.BlockSpec(memory_space=pltpu.VMEM)
-    tile16 = pltpu.VMEM((16, 8, 128), F32)
-    modes, spectrum = pl.pallas_call(
+    pieces = lambda count, rows: pltpu.VMEM((count, rows, 128), F32)
+    result = pl.pallas_call(
         kernel,
-        out_shape=(jax.ShapeDtypeStruct((R, PIECE), F32), jax.ShapeDtypeStruct((1, R), F32)),
+        out_shape=jax.ShapeDtypeStruct((32, 256), F32),
         in_specs=[pl.BlockSpec(memory_space=pl.ANY), vmem, vmem],
-        out_specs=(vmem, vmem),
+        out_specs=vmem,
         scratch_shapes=[
             pltpu.VMEM((128, LOCAL), BF16),
             pltpu.VMEM((128, 128), F32),
             pltpu.VMEM((2 * R, RP, 128), F32),
             pltpu.VMEM((RP, LOCAL), F32),
-            tile16, tile16, tile16,
+            pieces(8, 16), pieces(N_SPACE, 16), pieces(8, 16),
             pltpu.VMEM((G1, R, 640), F32),
             pltpu.VMEM((G1, R, 640), F32),
             pltpu.VMEM((256, 640), F32),
-            tile16, tile16, pltpu.VMEM((G1, 8, 128), F32), tile16,
+            pieces(7, 16), pieces(N_SPACE, 16), pieces(G1, 16), pieces(7, 16),
             pltpu.VMEM((RP, 640), F32),
             pltpu.VMEM((G2, R, 256), F32),
             pltpu.VMEM((G2, R, 256), F32),
             pltpu.VMEM((128, 256), F32),
-            tile16, tile16, pltpu.VMEM((N_TM, 8, 128), F32), tile16,
+            pieces(5, 8), pieces(N_SPACE, 8), pieces(N_TM, 8), pieces(5, 8),
             pltpu.SemaphoreType.DMA((X_PARTS,)),
             pltpu.SemaphoreType.DMA((N_TM,)),
             pltpu.SemaphoreType.DMA((10,)),
         ],
         compiler_params=pltpu.CompilerParams(collective_id=0, has_side_effects=True),
-    )(snapshots, start_block, merge_mix)
+    )(snapshots, start_block.T, merge_mix.T)
+    modes, spectrum = pl.pallas_call(
+        write_out,
+        out_shape=(jax.ShapeDtypeStruct((R, PIECE), F32), jax.ShapeDtypeStruct((1, R), F32)),
+        in_specs=[vmem],
+        out_specs=(vmem, vmem),
+    )(result)
     return modes, spectrum.reshape(R)
 
 

time: 86.4 us -> 76.5 us (0.89)
  local copies, waits for them, and re-layouts: 5.35 us -> 0 us
  Pallas kernels: 80.1 us -> 75.6 us
    unnamed x4 -> x0, local copies, waits for them, and re-layouts: 5.35 us -> none
    pallas_call x1 -> x2, Pallas kernels: 80.1 us -> 75.6 us  [the longest x1 74.2 us: local(): pl.pallas_call(kernel, out_shape=jax.ShapeDtypeStruct((32, 256), F32), in...]
where the time goes in v2:
time: 76.5 us; the launch traced here: 76.2 us
  Pallas kernels  75.6 us (99%)
    pallas_call x1, Pallas kernels, local(): pl.pallas_call(kernel, out_shape=jax.ShapeDtypeStruct((32, 256), F32), in...  74.2 us

profile of v2, /device:TPU:1, one launch (start us, length us, event | category | flops | bytes accessed | tf_op | source)
XLA Modules:
  0.0 76.2 jit_solution(16524027898908807159)
XLA Ops:
  0.6 74.2 %shard_map.50.result_ref = f32[32,256]{1,0:T(8,128)} custom-call(bf16[128,4608]{1,0:T(8,128)(2,1)} %x_hbm.1, f32[20,128]{1,0:T(8,128)} %bitcast.3, f32[20,40]{1,0:T(8,128)} %bitcast.4), custom_call_target="tpu_custom_call" | custom-call | tf_op jit(solution)/shard_map/pallas_call | solution.py:431
  74.8 1.4 %shard_map.51 = (f32[20,144]{1,0:T(8,128)}, f32[1,20]{1,0:T(1,128)}) custom-call(f32[32,256]{1,0:T(8,128)} %shard_map.50.result_ref), custom_call_target="tpu_custom_call" | custom-call | tf_op jit(solution)/shard_map/pallas_call | solution.py:457
